TPU v7x, 256 devices: a whole 4x4x8 slice. The times are simulated.
256 devices in a mesh: edge: 64 (over y, z, x_lo), chan: 4 (over x_hi, core).
Axes of the slice: x: 4 (x_hi: 2, x_lo: 2; x = x_hi * 2 + x_lo), y: 4, z: 8, core: 2. Of those that a mesh axis runs over, the one named last changes fastest.
Arguments:
- node_states: bfloat16 [1024, 49, 256], P('edge', None, 'chan'), may hold values from -6 to 6
- edge_vectors: float32 [3, 32768], P(None, ('edge', 'chan')), may hold values from -5.6 to 5.6, as said below
- source_part: int32 [32768, 1], P('edge'), may hold values from 0 to 63; in each aligned block of 512 rows (0 to 511, 512 to 1023, ...) at most 16 rows name the same one
- source_slot: int32 [32768], P('edge'), may hold values from 0 to 15
- target_slot: int32 [32768], P('edge'), may hold values from 0 to 15
- live_edges: int32 [64], P('edge'), may hold values from 1 to 512, 24576 in all
- weight_zero: bfloat16 [7, 256, 7, 256], P(None, 'chan'), may hold values from -0.125 to 0.125
- weight_one: bfloat16 [2, 6, 256, 6, 256], P(None, None, 'chan'), may hold values from -0.109375 to 0.109375
- weight_two: bfloat16 [2, 5, 256, 5, 256], P(None, None, 'chan'), may hold values from -0.125 to 0.125
Outputs:
- aggregated: bfloat16 [1024, 49, 256], P('edge', None, 'chan')
Inputs may be any that keep to these rules, and one draw needn't show every extreme that they name: `source_part`: in each aligned block of 512 rows (the edges of one partition's slab) no partition number appears more than 16 times, and some number appears exactly 16 times. Edges are grouped by destination partition: the destination of an edge in slab p is node p * 16 + target_slot. `live_edges`: live slots stand at the front of each slab; the fullest slab is full. `edge_vectors`: every column has length between 0.8 and 5.6.
All inputs are finite; a program needn't handle non-finite values. No bound on the sum of `live_edges` on one device may be relied on, other than what follows from the above.
Results may differ from a plain program's by a relative error of at most 0.015.
Values may be sent and summed in bfloat16 or wider, within the bound.
A program may use at most 128 MiB of HBM per device.

v0:
```python
import math
import jax
import jax.numpy as jnp
import numpy as np
from jax import lax
from jax.sharding import PartitionSpec as P

LMAX = 6
MMAX = 2
cutoff_radius = 6.0
highest = lax.Precision.HIGHEST


def harmonics(coord_x, coord_y, coord_z, degree_top, order_top):
    results = {}
    real_part = [coord_x * 0.0 + 1.0]
    imag_part = [coord_x * 0.0]
    for azimuthal in range(1, order_top + 1):
        new_real = coord_x * real_part[-1] - coord_y * imag_part[-1]
        new_imag = coord_x * imag_part[-1] + coord_y * real_part[-1]
        real_part.append(new_real)
        imag_part.append(new_imag)
    for azimuthal in range(order_top + 1):
        start_value = (-1.0) ** azimuthal * math.prod(range(2 * azimuthal - 1, 0, -2))
        legendre = {azimuthal: coord_z * 0.0 + start_value}
        if azimuthal + 1 <= degree_top:
            legendre[azimuthal + 1] = coord_z * ((2 * azimuthal + 1) * start_value)
        for degree in range(azimuthal + 2, degree_top + 1):
            legendre[degree] = (
                (2 * degree - 1) * coord_z * legendre[degree - 1]
                - (degree + azimuthal - 1) * legendre[degree - 2]
            ) / (degree - azimuthal)
        for degree in range(azimuthal, degree_top + 1):
            factor = math.sqrt(
                (2 * degree + 1)
                / (4.0 * math.pi)
                * math.factorial(degree - azimuthal)
                / math.factorial(degree + azimuthal)
            )
            if azimuthal == 0:
                results[degree, 0] = factor * legendre[degree]
            else:
                results[degree, azimuthal] = (
                    math.sqrt(2.0) * factor * legendre[degree] * real_part[azimuthal]
                )
                results[degree, -azimuthal] = (
                    math.sqrt(2.0) * factor * legendre[degree] * imag_part[azimuthal]
                )
    return results


def kept_rows():
    row_list = [(degree, 0) for degree in range(LMAX + 1)]
    for azimuthal in range(1, MMAX + 1):
        row_list += [(degree, azimuthal) for degree in range(azimuthal, LMAX + 1)]
        row_list += [(degree, -azimuthal) for degree in range(azimuthal, LMAX + 1)]
    return row_list


def row_offsets():
    listing = []
    offset = 0
    for degree, azimuthal in kept_rows():
        listing.append((degree, offset))
        offset += 2 * degree + 1
    return listing


def invert_small(matrix):
    order_size = matrix.shape[0]
    work = np.concatenate([matrix, np.eye(order_size)], axis=1)
    for column in range(order_size):
        work[column] = work[column] / work[column, column]
        for row_index in range(order_size):
            if row_index != column:
                work[row_index] = work[row_index] - work[row_index, column] * work[column]
    return work[:, order_size:]


def sample_tables():
    sample_count = 2 * (LMAX + 1) ** 2
    positions = np.arange(sample_count) + 0.5
    height = 1.0 - 2.0 * positions / sample_count
    radius = np.sqrt(1.0 - height * height)
    azimuth = math.pi * (3.0 - math.sqrt(5.0)) * positions
    points = np.stack([radius * np.cos(azimuth), radius * np.sin(azimuth), height])
    values = harmonics(points[0], points[1], points[2], LMAX, LMAX)
    inverses = []
    for degree in range(LMAX + 1):
        sampled = np.stack([values[degree, azimuthal] for azimuthal in range(-degree, degree + 1)])
        inverses.append(sampled.T @ invert_small(sampled @ sampled.T))
    return (points, inverses)


def wigner_rows(vectors):
    length = jnp.sqrt(jnp.sum(vectors * vectors, axis=0))
    direction = vectors / length
    pick_first = jnp.where(jnp.abs(direction[0]) < 0.6, 1.0, 0.0).astype(jnp.float32)
    helper = jnp.stack([pick_first, 1.0 - pick_first, jnp.zeros_like(pick_first)])
    first_axis = jnp.cross(direction, helper, axis=0)
    first_axis = first_axis / jnp.sqrt(jnp.sum(first_axis * first_axis, axis=0))
    second_axis = jnp.cross(direction, first_axis, axis=0)
    frames = jnp.stack([first_axis, second_axis, direction])
    points, inverses = sample_tables()
    sample = jnp.asarray(points, jnp.float32)
    turned = jnp.einsum("rce,ck->rek", frames, sample, precision=highest)
    values = harmonics(turned[0], turned[1], turned[2], LMAX, MMAX)
    pieces = []
    for degree, azimuthal in kept_rows():
        table = jnp.asarray(inverses[degree], jnp.float32)
        pieces.append(jnp.dot(values[degree, azimuthal], table, precision=highest))
    compact = jnp.concatenate(pieces, axis=1)
    envelope = 0.5 * (jnp.cos(math.pi * length / cutoff_radius) + 1.0)
    return (compact, envelope)


def rotate_forward(compact_t, sources):
    rows_out = []
    for degree, offset in row_offsets():
        total = compact_t[offset].astype(jnp.float32)[None, :] * sources[degree * degree].astype(
            jnp.float32
        )
        for inner in range(1, 2 * degree + 1):
            total = total + compact_t[offset + inner].astype(jnp.float32)[None, :] * sources[
                degree * degree + inner
            ].astype(jnp.float32)
        rows_out.append(total)
    return jnp.stack(rows_out, axis=0).astype(jnp.bfloat16)


def rotate_back(compact_t, scaled):
    listing = row_offsets()
    coefs_out = []
    for degree in range(LMAX + 1):
        for inner in range(2 * degree + 1):
            total = None
            for row_index, (row_degree, offset) in enumerate(listing):
                if row_degree == degree:
                    term = compact_t[offset + inner].astype(jnp.float32)[None, :] * scaled[
                        :, row_index
                    ].astype(jnp.float32)
                    total = term if total is None else total + term
            coefs_out.append(total)
    return jnp.stack(coefs_out, axis=0).astype(jnp.bfloat16)


def convolve(turned, weight_zero, weight_one, weight_two, contract):
    end_zero = LMAX + 1
    end_one_plus = end_zero + LMAX
    end_one_minus = end_one_plus + LMAX
    end_two_plus = end_one_minus + LMAX - 1
    zero_part = turned[:end_zero]
    one_plus = turned[end_zero:end_one_plus]
    one_minus = turned[end_one_plus:end_one_minus]
    two_plus = turned[end_one_minus:end_two_plus]
    two_minus = turned[end_two_plus:]
    pattern = "lce,lcjd->dje"
    out_zero = contract(pattern, zero_part, weight_zero)
    out_one_plus = contract(pattern, one_plus, weight_one[0]) - contract(
        pattern, one_minus, weight_one[1]
    )
    out_one_minus = contract(pattern, one_minus, weight_one[0]) + contract(
        pattern, one_plus, weight_one[1]
    )
    out_two_plus = contract(pattern, two_plus, weight_two[0]) - contract(
        pattern, two_minus, weight_two[1]
    )
    out_two_minus = contract(pattern, two_minus, weight_two[0]) + contract(
        pattern, two_plus, weight_two[1]
    )
    return jnp.concatenate(
        [out_zero, out_one_plus, out_one_minus, out_two_plus, out_two_minus], axis=1
    )


def mixed_contract(pattern, first_operand, second_operand):
    return jnp.einsum(pattern, first_operand, second_operand, preferred_element_type=jnp.float32)


def one_hot(indices, width):
    return (indices[:, None] == jnp.arange(width, dtype=jnp.int32)[None, :]).astype(jnp.bfloat16)


def pick_columns(table, selector):
    picked = lax.dot_general(
        table, selector, (((0,), (1,)), ((), ())), preferred_element_type=jnp.float32
    )
    return picked.astype(jnp.bfloat16)


def pick_rows(selector, table):
    return jnp.dot(selector, table, preferred_element_type=jnp.float32).astype(jnp.bfloat16)


def shards(
    node_states,
    edge_vectors,
    source_part,
    source_slot,
    target_slot,
    live_edges,
    weight_zero,
    weight_one,
    weight_two,
):
    slab_size = source_slot.shape[0]
    local_nodes = node_states.shape[0]
    local_channels = node_states.shape[2]
    coef_count = node_states.shape[1]
    group_count = lax.axis_size("edge")
    capacity = max(2, 2 * slab_size // group_count)
    slot_total = group_count * capacity
    quarter, quarter_fade = wigner_rows(edge_vectors)
    compact, envelope = (
        lax.all_gather(quarter.astype(jnp.bfloat16), "chan", axis=0, tiled=True),
        lax.all_gather(quarter_fade.astype(jnp.bfloat16), "chan", axis=0, tiled=True),
    )
    compact_t = compact.T
    node_flat = node_states.reshape(local_nodes, coef_count * local_channels)
    owner_part = source_part[:, 0]
    owners = jnp.arange(group_count, dtype=jnp.int32)
    member = (owner_part[:, None] == owners[None, :]).astype(jnp.int32)
    earlier = jnp.cumsum(member, axis=0) - member
    position = jnp.sum(earlier * member, axis=1)
    slot_flat = owner_part * capacity + position
    requests = (
        jnp.zeros((slot_total,), jnp.int32)
        .at[slot_flat]
        .set(source_slot)
        .reshape(group_count, capacity)
    )
    slot_select = one_hot(slot_flat, slot_total)
    wanted = lax.all_to_all(requests, "edge", split_axis=0, concat_axis=0, tiled=True)
    picked = pick_rows(one_hot(wanted.reshape(-1), local_nodes), node_flat)
    returned = lax.all_to_all(
        picked.reshape(group_count, capacity, coef_count * local_channels),
        "edge",
        split_axis=0,
        concat_axis=0,
        tiled=True,
    )
    sources = pick_columns(
        returned.reshape(slot_total, coef_count * local_channels), slot_select
    ).reshape(coef_count, local_channels, slab_size)
    turned = rotate_forward(compact_t, sources)
    channel_mix = lax.psum_scatter(
        convolve(turned, weight_zero, weight_one, weight_two, mixed_contract).astype(jnp.bfloat16),
        "chan",
        scatter_dimension=0,
        tiled=True,
    ).astype(jnp.float32)
    alive_mask = (jnp.arange(slab_size, dtype=jnp.int32) < live_edges[0]).astype(jnp.float32)
    scaling = envelope.astype(jnp.float32) * alive_mask
    scaled = (channel_mix * scaling).astype(jnp.bfloat16)
    message = rotate_back(compact_t, scaled).reshape(coef_count * local_channels, slab_size)
    selector = (jnp.arange(local_nodes, dtype=jnp.int32)[:, None] == target_slot[None, :]).astype(
        jnp.bfloat16
    )
    summed = lax.dot_general(
        selector, message, (((1,), (1,)), ((), ())), preferred_element_type=jnp.float32
    )
    return summed.astype(jnp.bfloat16).reshape(local_nodes, coef_count, local_channels)


def solution(mesh):
    in_specs = (
        P("edge", None, "chan"),
        P(None, ("edge", "chan")),
        P("edge", None),
        P("edge"),
        P("edge"),
        P("edge"),
        P(None, "chan", None, None),
        P(None, None, "chan", None, None),
        P(None, None, "chan", None, None),
    )
    out_specs = P("edge", None, "chan")
    return jax.shard_map(shards, mesh=mesh, in_specs=in_specs, out_specs=out_specs, check_vma=False)
```

profile of v0, /device:TPU:1, one launch (start us, length us, event | category | flops | bytes accessed | tf_op | source)
XLA Modules:
  0.0 345.9 jit_solution(5656310908398579439)
XLA Ops:
  7.4 1.2 reduce-window.6
  9.6 1.3 compare_select_fusion
  10.9 2.6 scatter_custom_fusion
  14.2 13.6 %all-to-all-start = ((s32[64,1,16]{2,1,0:T(1,128)}), s32[64,1,16]{2,1,0:T(1,128)S(1)}, u32[]{:S(2)}, u32[]{:S(2)}) async-start(s32[64,1,16]{2,1,0:T(1,128)} %bitcast.27), calls=%async_computation | async-start | bytes 65536 | tf_op jit(solution)/shard_map/all_to_all | solution.py:233
  29.7 7.3 %all-to-all-done = s32[64,1,16]{2,1,0:T(1,128)S(1)} async-done(((s32[64,1,16]{2,1,0:T(1,128)}), s32[64,1,16]{2,1,0:T(1,128)S(1)}, u32[]{:S(2)}, u32[]{:S(2)}) %all-to-all-start) | async-done | bytes 4128 | tf_op jit(solution)/shard_map/all_to_all | solution.py:233
  38.3 4.7 %convolution_convert_fusion = bf16[1024,3136]{0,1:T(8,128)(2,1)} fusion(bf16[16,3136]{1,0:T(8,128)(2,1)S(1)} %reshape.10748, s32[1024]{0:T(1024)S(1)} %eq.79), kind=kOutput, calls=%fused_computation.1 | convolution fusion | flops 105988096 | bytes 6526976 | tf_op jit(solution)/shard_map/dot_general | solution.py:192
  42.9 9.3 %copy.59 = bf16[1024,3136]{1,0:T(8,128)(2,1)} copy(bf16[1024,3136]{0,1:T(8,128)(2,1)} %convolution_convert_fusion) | data formatting | bytes 12845056 | tf_op jit(solution)/shard_map/convert_element_type | solution.py:192
  52.3 5.8 %all-to-all-start.1 = ((bf16[64,16,3136]{2,1,0:T(8,128)(2,1)}), bf16[64,16,3136]{2,1,0:T(8,128)(2,1)}, u32[]{:S(2)}, u32[]{:S(2)}) async-start(bf16[64,16,3136]{2,1,0:T(8,128)(2,1)} %bitcast.1286), calls=%async_computation.1 | async-start | bytes 13107200 | tf_op jit(solution)/shard_map/all_to_all | solution.py:235
  66.5 2.1 concatenate.16
  68.6 9.9 %all_gather.6 = bf16[512,235]{0,1:T(8,128)(2,1)S(1)} all-gather(bf16[128,235]{0,1:T(8,128)(2,1)S(1)} %concatenate.16), channel_id=1, replica_groups=mesh['edge'=64,'chan'=4] {'chan'}, dimensions={0}, use_global_device_ids=true | all-gather | bytes 300800 | tf_op jit(solution)/shard_map/all_gather | solution.py:215
  86.3 1.3 fusion.803
  87.6 1.2 fusion.802
  88.8 113.9 %all-to-all-done.1 = bf16[64,16,3136]{2,1,0:T(8,128)(2,1)} async-done(((bf16[64,16,3136]{2,1,0:T(8,128)(2,1)}), bf16[64,16,3136]{2,1,0:T(8,128)(2,1)}, u32[]{:S(2)}, u32[]{:S(2)}) %all-to-all-start.1) | async-done | bytes 6422560 | tf_op jit(solution)/shard_map/all_to_all | solution.py:235
  203.0 7.0 %convolution_convert_fusion.1 = bf16[3136,512]{1,0:T(8,128)(2,1)S(1)} fusion(bf16[1024,3136]{1,0:T(8,128)(2,1)} %bitcast.29, s32[512]{0:T(512)} %bitcast.1775), kind=kOutput, calls=%fused_computation.2 | convolution fusion | flops 3290464256 | bytes 9635840 | tf_op jit(solution)/shard_map/dot_general | solution.py:185
  213.7 1.0 fusion.12
  222.6 2.5 bitcast_dynamic-update-slice_fusion
  225.0 2.2 bitcast_dynamic-update-slice_fusion.2
  227.3 2.2 bitcast_dynamic-update-slice_fusion.1
  229.4 2.0 fusion.5
  231.4 1.9 fusion.7
  233.4 14.5 %copy.65 = bf16[256,29,512]{2,1,0:T(8,128)(2,1)} copy(bf16[256,29,512]{0,2,1:T(8,128)(2,1)} %fusion.7) | data formatting | bytes 15204352 | tf_op jit(solution)/shard_map/concatenate | solution.py:171
  248.5 9.3 %all-gather = bf16[4,1,128]{2,1,0:T(2,128)(2,1)S(1)} all-gather(bf16[1,1,128]{2,1,0:T(2,128)(2,1)S(1)} %copy-done.205), channel_id=1, replica_groups=mesh['edge'=64,'chan'=4] {'chan'}, dimensions={0}, use_global_device_ids=true | all-gather | bytes 1280 | tf_op jit(solution)/shard_map/all_gather | solution.py:216
  258.6 71.5 %reduce-scatter.2.cloned.1.call-done = bf16[64,29,512]{2,1,0:T(8,128)(2,1)} async-done(((bf16[256,29,512]{2,1,0:T(8,128)(2,1)}), bf16[64,29,512]{2,1,0:T(8,128)(2,1)}) %reduce-scatter.2.cloned.1.call-update) | async-done | bytes 1900560 | tf_op jit(solution)/shard_map/reduce_scatter | solution.py:246
  330.1 2.7 multiply_convert_fusion
  (574 shorter events, 37.2 us)
Async XLA Ops:
  6.5 216.0 %copy-start = (bf16[7,64,7,256]{3,1,2,0:T(8,128)(2,1)S(1)}, bf16[7,64,7,256]{3,1,2,0:T(8,128)(2,1)}, u32[]{:S(2)}) copy-start(bf16[7,64,7,256]{3,1,2,0:T(8,128)(2,1)} %param.47) | copy-start | bytes 4816900
  14.2 22.7 %all-to-all-start = ((s32[64,1,16]{2,1,0:T(1,128)}), s32[64,1,16]{2,1,0:T(1,128)S(1)}, u32[]{:S(2)}, u32[]{:S(2)}) async-start(s32[64,1,16]{2,1,0:T(1,128)} %bitcast.27), calls=%async_computation | async-start | bytes 65536 | tf_op jit(solution)/shard_map/all_to_all | solution.py:233
  52.3 150.4 %all-to-all-start.1 = ((bf16[64,16,3136]{2,1,0:T(8,128)(2,1)}), bf16[64,16,3136]{2,1,0:T(8,128)(2,1)}, u32[]{:S(2)}, u32[]{:S(2)}) async-start(bf16[64,16,3136]{2,1,0:T(8,128)(2,1)} %bitcast.1286), calls=%async_computation.1 | async-start | bytes 13107200 | tf_op jit(solution)/shard_map/all_to_all | solution.py:235
  58.1 272.0 %reduce-scatter.2.cloned.1.call-start = ((), (), s32[]{:S(2)}) async-start(), calls=%async_computation.3 | async-start | bytes 10485760 | tf_op jit(solution)/shard_map/reduce_scatter | solution.py:246
  62.2 24.0 %copy-start.3 = (bf16[2,5,64,5,256]{4,2,3,1,0:T(8,128)(2,1)S(1)}, bf16[2,5,64,5,256]{4,2,3,1,0:T(8,128)(2,1)}, u32[]{:S(2)}) copy-start(bf16[2,5,64,5,256]{4,2,3,1,0:T(8,128)(2,1)} %param.49) | copy-start | bytes 4915204
  68.5 19.0 %copy-start.2 = (bf16[2,6,64,6,256]{4,2,3,1,0:T(8,128)(2,1)S(1)}, bf16[2,6,64,6,256]{4,2,3,1,0:T(8,128)(2,1)}, u32[]{:S(2)}) copy-start(bf16[2,6,64,6,256]{4,2,3,1,0:T(8,128)(2,1)} %param.48) | copy-start | bytes 7077892
  247.9 85.1 %copy-start.164 = (f32[1,512]{1,0:T(1,128)S(1)}, f32[1,512]{1,0:T(1,128)}, u32[]{:S(2)}) copy-start(f32[1,512]{1,0:T(1,128)} %get-tuple-element.162) | copy-start | bytes 6148
  247.9 85.1 %copy-start.201 = (f32[1,512]{1,0:T(1,128)S(1)}, f32[1,512]{1,0:T(1,128)}, u32[]{:S(2)}) copy-start(f32[1,512]{1,0:T(1,128)} %get-tuple-element.208) | copy-start | bytes 6148
  247.9 85.2 %copy-start.158 = (f32[1,512]{1,0:T(1,128)S(1)}, f32[1,512]{1,0:T(1,128)}, u32[]{:S(2)}) copy-start(f32[1,512]{1,0:T(1,128)} %get-tuple-element.161) | copy-start | bytes 6148
  247.9 85.2 %copy-start.199 = (f32[1,512]{1,0:T(1,128)S(1)}, f32[1,512]{1,0:T(1,128)}, u32[]{:S(2)}) copy-start(f32[1,512]{1,0:T(1,128)} %get-tuple-element.210) | copy-start | bytes 6148
  247.9 85.2 %copy-start.152 = (f32[1,512]{1,0:T(1,128)S(1)}, f32[1,512]{1,0:T(1,128)}, u32[]{:S(2)}) copy-start(f32[1,512]{1,0:T(1,128)} %get-tuple-element.160) | copy-start | bytes 6148
  247.9 85.2 %copy-start.198 = (f32[1,512]{1,0:T(1,128)S(1)}, f32[1,512]{1,0:T(1,128)}, u32[]{:S(2)}) copy-start(f32[1,512]{1,0:T(1,128)} %get-tuple-element.209) | copy-start | bytes 6148
  247.9 85.3 %copy-start.144 = (f32[1,512]{1,0:T(1,128)S(1)}, f32[1,512]{1,0:T(1,128)}, u32[]{:S(2)}) copy-start(f32[1,512]{1,0:T(1,128)} %get-tuple-element.159) | copy-start | bytes 6148
  248.0 85.3 %copy-start.202 = (f32[1,512]{1,0:T(1,128)S(1)}, f32[1,512]{1,0:T(1,128)}, u32[]{:S(2)}) copy-start(f32[1,512]{1,0:T(1,128)} %get-tuple-element.207) | copy-start | bytes 6148
  248.0 85.4 %copy-start.134 = (f32[1,512]{1,0:T(1,128)S(1)}, f32[1,512]{1,0:T(1,128)}, u32[]{:S(2)}) copy-start(f32[1,512]{1,0:T(1,128)} %get-tuple-element.158) | copy-start | bytes 6148
  248.0 85.4 %copy-start.200 = (f32[1,512]{1,0:T(1,128)S(1)}, f32[1,512]{1,0:T(1,128)}, u32[]{:S(2)}) copy-start(f32[1,512]{1,0:T(1,128)} %get-tuple-element.206) | copy-start | bytes 6148
  248.0 85.5 %copy-start.126 = (f32[1,512]{1,0:T(1,128)S(1)}, f32[1,512]{1,0:T(1,128)}, u32[]{:S(2)}) copy-start(f32[1,512]{1,0:T(1,128)} %get-tuple-element.157) | copy-start | bytes 6148
  248.0 85.5 %copy-start.197 = (f32[1,512]{1,0:T(1,128)S(1)}, f32[1,512]{1,0:T(1,128)}, u32[]{:S(2)}) copy-start(f32[1,512]{1,0:T(1,128)} %get-tuple-element.205) | copy-start | bytes 6148
  248.0 85.6 %copy-start.196 = (f32[1,512]{1,0:T(1,128)S(1)}, f32[1,512]{1,0:T(1,128)}, u32[]{:S(2)}) copy-start(f32[1,512]{1,0:T(1,128)} %get-tuple-element.204) | copy-start | bytes 6148
  258.5 75.2 %copy-start.193 = (f32[1,512]{1,0:T(1,128)S(1)}, f32[1,512]{1,0:T(1,128)}, u32[]{:S(2)}) copy-start(f32[1,512]{1,0:T(1,128)} %get-tuple-element.203) | copy-start | bytes 6148
  258.5 75.3 %copy-start.190 = (f32[1,512]{1,0:T(1,128)S(1)}, f32[1,512]{1,0:T(1,128)}, u32[]{:S(2)}) copy-start(f32[1,512]{1,0:T(1,128)} %get-tuple-element.202) | copy-start | bytes 6148
  258.5 75.4 %copy-start.187 = (f32[1,512]{1,0:T(1,128)S(1)}, f32[1,512]{1,0:T(1,128)}, u32[]{:S(2)}) copy-start(f32[1,512]{1,0:T(1,128)} %get-tuple-element.201) | copy-start | bytes 6148
  258.5 75.4 %copy-start.183 = (f32[1,512]{1,0:T(1,128)S(1)}, f32[1,512]{1,0:T(1,128)}, u32[]{:S(2)}) copy-start(f32[1,512]{1,0:T(1,128)} %get-tuple-element.200) | copy-start | bytes 6148
  258.6 75.5 %copy-start.178 = (f32[1,512]{1,0:T(1,128)S(1)}, f32[1,512]{1,0:T(1,128)}, u32[]{:S(2)}) copy-start(f32[1,512]{1,0:T(1,128)} %get-tuple-element.199) | copy-start | bytes 6148
  (189 other events, 623.1 us)
Sparse Core Ops, SparseCore 0:
  248.0 82.0 reduce-scatter.1
where the time goes:
time: 347 us; the launch traced here: 346 us
  waiting for transfers between devices  193 us (56%)
  local copies, waits for them, and re-layouts  35.9 us (10%)
  matrix products  34.4 us (10%)
  other arithmetic  26.4 us (8%)
  starting transfers between devices  19.5 us (6%)
  blocking collectives  19.2 us (6%)
  between operations  17.8 us (5%)
    all_to_all x1, waiting for transfers between devices, shards(): lax.all_to_all(picked.reshape(group_count, capacity, coef_count * local_c...  114 us
    reduce_scatter x1, waiting for transfers between devices, shards(): lax.psum_scatter(convolve(turned, weight_zero, weight_one, weight_two, mi...  71.5 us
    dot_general x9, matrix products, mixed_contract(): jnp.einsum(pattern, first_operand, second_operand, preferred_element_type...  14.5 us
    concatenate x1, local copies, waits for them, and re-layouts, convolve(): jnp.concatenate([out_zero, out_one_plus, out_one_minus, out_two_plus, out...  14.5 us
    all_to_all x1, starting transfers between devices, shards(): lax.all_to_all(requests, 'edge', split_axis=0, concat_axis=0, tiled=True)  13.6 us
    all_gather x1, blocking collectives, shards(): lax.all_gather(quarter.astype(jnp.bfloat16), 'chan', axis=0, tiled=True)  9.89 us
    all_gather x1, blocking collectives, shards(): lax.all_gather(quarter_fade.astype(jnp.bfloat16), 'chan', axis=0, tiled=T...  9.35 us
    convert_element_type x1, local copies, waits for them, and re-layouts, pick_rows(): jnp.dot(selector, table, preferred_element_type=jnp.float32)  9.26 us
  transfers between devices with their start and end apart: 3, of which 3 were waited for; matrix products, arithmetic and copies ran while one was open for 6% of the time, Pallas kernels for 0%

commit v1 on v0

--- a/solution.py
+++ b/solution.py
@@ -213,7 +213,12 @@
     quarter, quarter_fade = wigner_rows(edge_vectors)
     compact, envelope = (
         lax.all_gather(quarter.astype(jnp.bfloat16), "chan", axis=0, tiled=True),
-        lax.all_gather(quarter_fade.astype(jnp.bfloat16), "chan", axis=0, tiled=True),
+        jnp.concatenate(
+            lax.all_to_all(
+                jnp.stack([quarter_fade.astype(jnp.bfloat16)] * lax.axis_size("chan")), "chan", 0, 0
+            ),
+            axis=0,
+        ),
     )
     compact_t = compact.T
     node_flat = node_states.reshape(local_nodes, coef_count * local_channels)

time: 347 us -> 347 us (level)
  blocking collectives: 19.2 us -> 9.91 us
  starting transfers between devices: 19.5 us -> 26.4 us
    all_gather x1 -> x0, blocking collectives: 9.35 us -> none  [shards(): lax.all_gather(quarter_fade.astype(jnp.bfloat16), 'chan', axis=0, tiled=T...]
    all_to_all x0 -> x1, starting transfers between devices: none -> 6.96 us  [shards(): lax.all_to_all(jnp.stack([quarter_fade.astype(jnp.bfloat16)] * lax.axis_s...]
    all_to_all x0 -> x1, waiting for transfers between devices: none -> 3.87 us  [shards(): lax.all_to_all(jnp.stack([quarter_fade.astype(jnp.bfloat16)] * lax.axis_s...]
    unnamed x69 -> x68, other arithmetic: 9.1 us -> 8.5 us
  transfers between devices with their start and end apart: 3 -> 4, of which waited for: 3 -> 4; matrix products, arithmetic and copies ran while one was open for 6% -> 7% of each run, Pallas kernels for 0% -> 0%
where the time goes in v1:
time: 347 us; the launch traced here: 346 us
  waiting for transfers between devices  195 us (56%)
  local copies, waits for them, and re-layouts  36.2 us (10%)
  matrix products  34.4 us (10%)
  other arithmetic  26.4 us (8%)
  starting transfers between devices  26.4 us (8%)
  between operations  17.7 us (5%)
  blocking collectives  9.91 us (3%)
    all_to_all x1, waiting for transfers between devices, shards(): lax.all_to_all(picked.reshape(group_count, capacity, coef_count * local_c...  114 us
    reduce_scatter x1, waiting for transfers between devices, shards(): lax.psum_scatter(convolve(turned, weight_zero, weight_one, weight_two, mi...  69.5 us
    dot_general x9, matrix products, mixed_contract(): jnp.einsum(pattern, first_operand, second_operand, preferred_element_type...  14.5 us
    concatenate x1, local copies, waits for them, and re-layouts, convolve(): jnp.concatenate([out_zero, out_one_plus, out_one_minus, out_two_plus, out...  14.5 us
    all_to_all x1, starting transfers between devices, shards(): lax.all_to_all(requests, 'edge', split_axis=0, concat_axis=0, tiled=True)  13.6 us
    all_gather x1, blocking collectives, shards(): lax.all_gather(quarter.astype(jnp.bfloat16), 'chan', axis=0, tiled=True)  9.91 us
    convert_element_type x1, local copies, waits for them, and re-layouts, pick_rows(): jnp.dot(selector, table, preferred_element_type=jnp.float32)  9.05 us
    unnamed x68, other arithmetic  8.5 us
  transfers between devices with their start and end apart: 4, of which 4 were waited for; matrix products, arithmetic and copies ran while one was open for 7% of the time, Pallas kernels for 0%

profile of v1, /device:TPU:1, one launch (start us, length us, event | category | flops | bytes accessed | tf_op | source)
XLA Modules:
  0.0 345.7 jit_solution(17183697845819492272)
XLA Ops:
  7.4 1.2 reduce-window.6
  9.6 1.3 compare_select_fusion
  10.9 2.6 scatter_custom_fusion
  14.2 13.6 %all-to-all-start = ((s32[64,1,16]{2,1,0:T(1,128)}), s32[64,1,16]{2,1,0:T(1,128)S(1)}, u32[]{:S(2)}, u32[]{:S(2)}) async-start(s32[64,1,16]{2,1,0:T(1,128)} %bitcast.27), calls=%async_computation | async-start | bytes 65536 | tf_op jit(solution)/shard_map/all_to_all | solution.py:238
  29.7 7.3 %all-to-all-done = s32[64,1,16]{2,1,0:T(1,128)S(1)} async-done(((s32[64,1,16]{2,1,0:T(1,128)}), s32[64,1,16]{2,1,0:T(1,128)S(1)}, u32[]{:S(2)}, u32[]{:S(2)}) %all-to-all-start) | async-done | bytes 4128 | tf_op jit(solution)/shard_map/all_to_all | solution.py:238
  38.3 4.7 %convolution_convert_fusion = bf16[1024,3136]{0,1:T(8,128)(2,1)} fusion(bf16[16,3136]{1,0:T(8,128)(2,1)S(1)} %reshape.10767, s32[1024]{0:T(1024)S(1)} %eq.79), kind=kOutput, calls=%fused_computation.1 | convolution fusion | flops 105988096 | bytes 6526976 | tf_op jit(solution)/shard_map/dot_general | solution.py:192
  43.0 9.1 %copy.59 = bf16[1024,3136]{1,0:T(8,128)(2,1)} copy(bf16[1024,3136]{0,1:T(8,128)(2,1)} %convolution_convert_fusion) | data formatting | bytes 12845056 | tf_op jit(solution)/shard_map/convert_element_type | solution.py:192
  52.1 5.9 %all-to-all-start.1 = ((bf16[64,16,3136]{2,1,0:T(8,128)(2,1)}), bf16[64,16,3136]{2,1,0:T(8,128)(2,1)}, u32[]{:S(2)}, u32[]{:S(2)}) async-start(bf16[64,16,3136]{2,1,0:T(8,128)(2,1)} %bitcast.1284), calls=%async_computation.1 | async-start | bytes 13107200 | tf_op jit(solution)/shard_map/all_to_all | solution.py:240
  66.3 2.1 concatenate.16
  68.3 9.9 %all_gather.3 = bf16[512,235]{0,1:T(8,128)(2,1)S(1)} all-gather(bf16[128,235]{0,1:T(8,128)(2,1)S(1)} %concatenate.16), channel_id=1, replica_groups=mesh['edge'=64,'chan'=4] {'chan'}, dimensions={0}, use_global_device_ids=true | all-gather | bytes 300800 | tf_op jit(solution)/shard_map/all_gather | solution.py:215
  86.1 1.3 fusion.803
  87.4 1.2 fusion.802
  88.6 113.9 %all-to-all-done.1 = bf16[64,16,3136]{2,1,0:T(8,128)(2,1)} async-done(((bf16[64,16,3136]{2,1,0:T(8,128)(2,1)}), bf16[64,16,3136]{2,1,0:T(8,128)(2,1)}, u32[]{:S(2)}, u32[]{:S(2)}) %all-to-all-start.1) | async-done | bytes 6422560 | tf_op jit(solution)/shard_map/all_to_all | solution.py:240
  202.8 7.0 %convolution_convert_fusion.1 = bf16[3136,512]{1,0:T(8,128)(2,1)S(1)} fusion(bf16[1024,3136]{1,0:T(8,128)(2,1)} %bitcast.29, s32[512]{0:T(512)} %bitcast.1773), kind=kOutput, calls=%fused_computation.2 | convolution fusion | flops 3290464256 | bytes 9635840 | tf_op jit(solution)/shard_map/dot_general | solution.py:185
  222.4 2.5 bitcast_dynamic-update-slice_fusion
  224.9 2.2 bitcast_dynamic-update-slice_fusion.2
  227.1 2.2 bitcast_dynamic-update-slice_fusion.1
  229.3 2.0 fusion.5
  231.2 1.9 fusion.7
  233.2 14.5 %copy.65 = bf16[256,29,512]{2,1,0:T(8,128)(2,1)} copy(bf16[256,29,512]{0,2,1:T(8,128)(2,1)} %fusion.7) | data formatting | bytes 15204352 | tf_op jit(solution)/shard_map/concatenate | solution.py:171
  248.9 7.0 %all-to-all-start.2 = ((bf16[4,1,128]{2,1,0:T(2,128)(2,1)}), bf16[4,1,128]{2,1,0:T(2,128)(2,1)S(1)}, u32[]{:S(2)}, u32[]{:S(2)}) async-start(bf16[4,1,128]{2,1,0:T(2,128)(2,1)} %stack.36), calls=%async_computation.3 | async-start | bytes 4096 | tf_op jit(solution)/shard_map/all_to_all | solution.py:217
  256.5 3.9 %all-to-all-done.2 = bf16[4,1,128]{2,1,0:T(2,128)(2,1)S(1)} async-done(((bf16[4,1,128]{2,1,0:T(2,128)(2,1)}), bf16[4,1,128]{2,1,0:T(2,128)(2,1)S(1)}, u32[]{:S(2)}, u32[]{:S(2)}) %all-to-all-start.2) | async-done | bytes 1056 | tf_op jit(solution)/shard_map/all_to_all | solution.py:217
  260.4 69.5 %reduce-scatter.2.cloned.1.call-done = bf16[64,29,512]{2,1,0:T(8,128)(2,1)} async-done(((bf16[256,29,512]{2,1,0:T(8,128)(2,1)}), bf16[64,29,512]{2,1,0:T(8,128)(2,1)}) %reduce-scatter.2.cloned.1.call-update) | async-done | bytes 1900560 | tf_op jit(solution)/shard_map/reduce_scatter | solution.py:251
  330.0 2.7 multiply_convert_fusion
  (576 shorter events, 38.7 us)
Async XLA Ops:
  6.5 215.9 %copy-start = (bf16[7,64,7,256]{3,1,2,0:T(8,128)(2,1)S(1)}, bf16[7,64,7,256]{3,1,2,0:T(8,128)(2,1)}, u32[]{:S(2)}) copy-start(bf16[7,64,7,256]{3,1,2,0:T(8,128)(2,1)} %param.47) | copy-start | bytes 4816900
  14.2 22.7 %all-to-all-start = ((s32[64,1,16]{2,1,0:T(1,128)}), s32[64,1,16]{2,1,0:T(1,128)S(1)}, u32[]{:S(2)}, u32[]{:S(2)}) async-start(s32[64,1,16]{2,1,0:T(1,128)} %bitcast.27), calls=%async_computation | async-start | bytes 65536 | tf_op jit(solution)/shard_map/all_to_all | solution.py:238
  52.1 150.4 %all-to-all-start.1 = ((bf16[64,16,3136]{2,1,0:T(8,128)(2,1)}), bf16[64,16,3136]{2,1,0:T(8,128)(2,1)}, u32[]{:S(2)}, u32[]{:S(2)}) async-start(bf16[64,16,3136]{2,1,0:T(8,128)(2,1)} %bitcast.1284), calls=%async_computation.1 | async-start | bytes 13107200 | tf_op jit(solution)/shard_map/all_to_all | solution.py:240
  57.9 272.0 %reduce-scatter.2.cloned.1.call-start = ((), (), s32[]{:S(2)}) async-start(), calls=%async_computation.4 | async-start | bytes 10485760 | tf_op jit(solution)/shard_map/reduce_scatter | solution.py:251
  62.0 24.0 %copy-start.3 = (bf16[2,5,64,5,256]{4,2,3,1,0:T(8,128)(2,1)S(1)}, bf16[2,5,64,5,256]{4,2,3,1,0:T(8,128)(2,1)}, u32[]{:S(2)}) copy-start(bf16[2,5,64,5,256]{4,2,3,1,0:T(8,128)(2,1)} %param.49) | copy-start | bytes 4915204
  247.7 85.1 %copy-start.164 = (f32[1,512]{1,0:T(1,128)S(1)}, f32[1,512]{1,0:T(1,128)}, u32[]{:S(2)}) copy-start(f32[1,512]{1,0:T(1,128)} %get-tuple-element.162) | copy-start | bytes 6148
  247.7 85.1 %copy-start.201 = (f32[1,512]{1,0:T(1,128)S(1)}, f32[1,512]{1,0:T(1,128)}, u32[]{:S(2)}) copy-start(f32[1,512]{1,0:T(1,128)} %get-tuple-element.208) | copy-start | bytes 6148
  247.7 85.2 %copy-start.158 = (f32[1,512]{1,0:T(1,128)S(1)}, f32[1,512]{1,0:T(1,128)}, u32[]{:S(2)}) copy-start(f32[1,512]{1,0:T(1,128)} %get-tuple-element.161) | copy-start | bytes 6148
  247.7 85.2 %copy-start.199 = (f32[1,512]{1,0:T(1,128)S(1)}, f32[1,512]{1,0:T(1,128)}, u32[]{:S(2)}) copy-start(f32[1,512]{1,0:T(1,128)} %get-tuple-element.210) | copy-start | bytes 6148
  247.7 85.2 %copy-start.152 = (f32[1,512]{1,0:T(1,128)S(1)}, f32[1,512]{1,0:T(1,128)}, u32[]{:S(2)}) copy-start(f32[1,512]{1,0:T(1,128)} %get-tuple-element.160) | copy-start | bytes 6148
  247.8 85.2 %copy-start.198 = (f32[1,512]{1,0:T(1,128)S(1)}, f32[1,512]{1,0:T(1,128)}, u32[]{:S(2)}) copy-start(f32[1,512]{1,0:T(1,128)} %get-tuple-element.209) | copy-start | bytes 6148
  247.8 85.3 %copy-start.144 = (f32[1,512]{1,0:T(1,128)S(1)}, f32[1,512]{1,0:T(1,128)}, u32[]{:S(2)}) copy-start(f32[1,512]{1,0:T(1,128)} %get-tuple-element.159) | copy-start | bytes 6148
  247.8 85.3 %copy-start.202 = (f32[1,512]{1,0:T(1,128)S(1)}, f32[1,512]{1,0:T(1,128)}, u32[]{:S(2)}) copy-start(f32[1,512]{1,0:T(1,128)} %get-tuple-element.207) | copy-start | bytes 6148
  247.8 85.4 %copy-start.134 = (f32[1,512]{1,0:T(1,128)S(1)}, f32[1,512]{1,0:T(1,128)}, u32[]{:S(2)}) copy-start(f32[1,512]{1,0:T(1,128)} %get-tuple-element.158) | copy-start | bytes 6148
  247.8 85.4 %copy-start.200 = (f32[1,512]{1,0:T(1,128)S(1)}, f32[1,512]{1,0:T(1,128)}, u32[]{:S(2)}) copy-start(f32[1,512]{1,0:T(1,128)} %get-tuple-element.206) | copy-start | bytes 6148
  247.8 85.5 %copy-start.126 = (f32[1,512]{1,0:T(1,128)S(1)}, f32[1,512]{1,0:T(1,128)}, u32[]{:S(2)}) copy-start(f32[1,512]{1,0:T(1,128)} %get-tuple-element.157) | copy-start | bytes 6148
  247.8 85.5 %copy-start.197 = (f32[1,512]{1,0:T(1,128)S(1)}, f32[1,512]{1,0:T(1,128)}, u32[]{:S(2)}) copy-start(f32[1,512]{1,0:T(1,128)} %get-tuple-element.205) | copy-start | bytes 6148
  247.8 85.6 %copy-start.196 = (f32[1,512]{1,0:T(1,128)S(1)}, f32[1,512]{1,0:T(1,128)}, u32[]{:S(2)}) copy-start(f32[1,512]{1,0:T(1,128)} %get-tuple-element.204) | copy-start | bytes 6148
  248.9 11.5 %all-to-all-start.2 = ((bf16[4,1,128]{2,1,0:T(2,128)(2,1)}), bf16[4,1,128]{2,1,0:T(2,128)(2,1)S(1)}, u32[]{:S(2)}, u32[]{:S(2)}) async-start(bf16[4,1,128]{2,1,0:T(2,128)(2,1)} %stack.36), calls=%async_computation.3 | async-start | bytes 4096 | tf_op jit(solution)/shard_map/all_to_all | solution.py:217
  260.4 73.2 %copy-start.193 = (f32[1,512]{1,0:T(1,128)S(1)}, f32[1,512]{1,0:T(1,128)}, u32[]{:S(2)}) copy-start(f32[1,512]{1,0:T(1,128)} %get-tuple-element.203) | copy-start | bytes 6148
  260.4 73.3 %copy-start.190 = (f32[1,512]{1,0:T(1,128)S(1)}, f32[1,512]{1,0:T(1,128)}, u32[]{:S(2)}) copy-start(f32[1,512]{1,0:T(1,128)} %get-tuple-element.202) | copy-start | bytes 6148
  260.4 73.4 %copy-start.187 = (f32[1,512]{1,0:T(1,128)S(1)}, f32[1,512]{1,0:T(1,128)}, u32[]{:S(2)}) copy-start(f32[1,512]{1,0:T(1,128)} %get-tuple-element.201) | copy-start | bytes 6148
  260.4 73.4 %copy-start.183 = (f32[1,512]{1,0:T(1,128)S(1)}, f32[1,512]{1,0:T(1,128)}, u32[]{:S(2)}) copy-start(f32[1,512]{1,0:T(1,128)} %get-tuple-element.200) | copy-start | bytes 6148
  260.4 73.5 %copy-start.178 = (f32[1,512]{1,0:T(1,128)S(1)}, f32[1,512]{1,0:T(1,128)}, u32[]{:S(2)}) copy-start(f32[1,512]{1,0:T(1,128)} %get-tuple-element.199) | copy-start | bytes 6148
  (190 other events, 641.8 us)
Sparse Core Ops, SparseCore 0:
  247.8 82.0 reduce-scatter.1
